TPU v7x, 32 devices: a whole 2x2x4 slice. The times are simulated.
32 devices in a mesh: grp: 2 (over x), row: 16 (over z, y, core).
Axes of the slice: x: 2, y: 2, z: 4, core: 2. Of those that a mesh axis runs over, the one named last changes fastest.
Arguments:
- kmesh: int32 [32, 3], P(('grp', 'row')), parts along dimension 0, may hold values from 0 to 15
- rcoord: int32 [768, 3], P(('grp', 'row')), parts along dimension 0, may hold values from -8 to 8
- degen: int32 [768], P(('grp', 'row')), parts along dimension 0, may hold values from 1 to 4
- hr_re: float32 [768, 128, 128], P(('grp', 'row')), parts along dimension 0, may hold values from -1.5 to 1.5
- hr_im: float32 [768, 128, 128], P(('grp', 'row')), parts along dimension 0, may hold values from -1.5 to 1.5
Outputs:
- hk_re: float32 [32, 128, 128], P(('grp', 'row')), parts along dimension 0
- hk_im: float32 [32, 128, 128], P(('grp', 'row')), parts along dimension 0
There are 2 independent parts, one for each index of `grp`. A program takes and returns all parts, laid end to end along the dimension named above; each array names one. Nothing has to cross between parts.
All inputs are finite; a program needn't handle non-finite values.
Results may differ from a plain program's by a relative error of at most 0.00007.
Values sent between devices are 32-bit elements; how exact they have to be, the bound alone decides.
No kernel may reach another device: no remote copies, remote signals or barrier semaphores. Data moves between devices by JAX's collectives and lax.ppermute only.
A program may use at most 64 MiB of HBM per device.

v0:
```python
import math
import jax
import jax.numpy as jnp
from jax import lax
from jax.sharding import PartitionSpec as P

MESH = 16


def phase_terms(kblock, coords, inverse, real_flat, imag_flat):
    highest = lax.Precision.HIGHEST
    prod = jnp.sum(kblock[:, None, :] * coords[None, :, :], axis=-1)
    phase = jnp.mod(prod, MESH)
    angle = phase.astype(jnp.float32) * (2.0 * math.pi / MESH)
    cosine = jnp.cos(angle) * inverse[None, :]
    sine = jnp.sin(angle) * inverse[None, :]
    part_re = jnp.dot(
        cosine, real_flat, precision=highest, preferred_element_type=jnp.float32
    ) - jnp.dot(sine, imag_flat, precision=highest, preferred_element_type=jnp.float32)
    part_im = jnp.dot(
        sine, real_flat, precision=highest, preferred_element_type=jnp.float32
    ) + jnp.dot(cosine, imag_flat, precision=highest, preferred_element_type=jnp.float32)
    return (part_re, part_im)


def shards(kmesh, rcoord, degen, hr_re, hr_im):
    width = hr_re.shape[1]
    every_k = lax.all_gather(kmesh, "row", axis=0, tiled=True)
    total_k = every_k.shape[0]
    local_r = hr_re.shape[0]
    real_flat = hr_re.reshape(local_r, -1)
    imag_flat = hr_im.reshape(local_r, -1)
    inverse = 1.0 / degen.astype(jnp.float32)
    part_re, part_im = phase_terms(every_k, rcoord, inverse, real_flat, imag_flat)
    whole = jnp.concatenate([part_re, part_im], axis=1).reshape(total_k, 2, width, width)
    by_rows = lax.psum_scatter(whole, "row", scatter_dimension=2, tiled=True)
    mine = lax.all_to_all(by_rows, "row", split_axis=0, concat_axis=2, tiled=True)
    return (mine[:, 0], mine[:, 1])


def solution(mesh):
    placed = (
        P(("grp", "row"), None),
        P(("grp", "row"), None),
        P(("grp", "row")),
        P(("grp", "row"), None, None),
        P(("grp", "row"), None, None),
    )
    return jax.shard_map(
        shards,
        mesh=mesh,
        in_specs=placed,
        out_specs=(P(("grp", "row"), None, None), P(("grp", "row"), None, None)),
        check_vma=False,
    )
```

profile of v0, /device:TPU:0, one launch (start us, length us, event | category | flops | bytes accessed | tf_op | source)
XLA Modules:
  0.0 121.5 jit_solution(16764732116881558362)
XLA Ops:
  7.2 0.0 copy-start
  7.2 0.0 reduce-scatter.2.cloned.1.call-start
  7.2 0.8 convert_divide_fusion
  8.0 23.3 %all-gather = s32[16,1,3]{2,1,0:T(1,128)S(1)} all-gather(s32[1,1,3]{2,1,0:T(1,128)} %bitcast.35), channel_id=1, replica_groups=mesh['grp'=2,'row'=16] {'row'}, dimensions={0}, use_global_device_ids=true | all-gather | bytes 204 | tf_op jit(solution)/shard_map/all_gather | solution.py:28
  31.3 0.1 copy.15
  31.4 0.8 multiply_reduce_fusion
  32.1 3.3 %fusion.2 = f32[16,16384]{1,0:T(8,128)S(1)} fusion(f32[3,8,128,128]{3,2,1,0:T(8,128)} %bitcast.30, f32[24]{0:T(128)S(1)} %convert_divide_fusion, s32[16,24]{1,0:T(8,128)S(1)} %multiply_reduce_fusion), kind=kOutput, calls=%fused_computation.5 | convolution fusion | flops 75502848 | bytes 2623072 | tf_op jit(solution)/shard_map/dot_general | solution.py:20
  35.4 0.0 copy-done
  35.4 0.0 copy-start.1
  35.4 1.9 %fusion.4 = f32[16,16384]{1,0:T(8,128)S(1)} fusion(f32[3,8,128,128]{3,2,1,0:T(8,128)S(1)} %bitcast.31, f32[24]{0:T(128)S(1)} %convert_divide_fusion, s32[16,24]{1,0:T(8,128)S(1)} %multiply_reduce_fusion), kind=kOutput, calls=%fused_computation.7 | convolution fusion | flops 75502848 | bytes 2623072 | tf_op jit(solution)/shard_map/dot_general | solution.py:17
  37.4 0.0 copy-done.1
  37.4 1.9 %convolution_add_fusion = f32[16,16384]{1,0:T(8,128)S(1)} fusion(f32[16,16384]{1,0:T(8,128)S(1)} %fusion.2, f32[3,8,128,128]{3,2,1,0:T(8,128)S(1)} %bitcast.32, f32[24]{0:T(128)S(1)} %convert_divide_fusion, s32[16,24]{1,0:T(8,128)S(1)} %multiply_reduce_fusion), kind=kOutput, calls=%fused_computation | convolution fusion | flops 75764992 | bytes 3671648 | tf_op jit(solution)/shard_map/dot_general | solution.py:22
  39.3 1.9 %convolution_subtract_fusion = f32[16,16384]{1,0:T(8,128)S(1)} fusion(f32[16,16384]{1,0:T(8,128)S(1)} %fusion.4, f32[3,8,128,128]{3,2,1,0:T(8,128)S(1)} %bitcast.33, f32[24]{0:T(128)S(1)} %convert_divide_fusion, s32[16,24]{1,0:T(8,128)S(1)} %multiply_reduce_fusion), kind=kOutput, calls=%fused_computation.1 | convolution fusion | flops 75764992 | bytes 3671648 | tf_op jit(solution)/shard_map/dot_general | solution.py:19
  41.2 0.1 maximum_bitcast_fusion
  41.4 1.8 %copy.19 = f32[2,8,256,128]{3,2,1,0:T(8,128)} copy(f32[2,8,256,128]{3,1,2,0:T(8,128)S(1)} %maximum_bitcast_fusion) | data formatting | bytes 4194304
  43.1 0.0 reduce-scatter.2.cloned.1.call-update
  43.2 59.2 %reduce-scatter.2.cloned.1.call-done = f32[16,2,8,128]{3,2,1,0:T(8,128)} async-done(((f32[16,2,128,128]{3,2,1,0:T(8,128)}), f32[16,2,8,128]{3,2,1,0:T(8,128)}) %reduce-scatter.2.cloned.1.call-update) | async-done | bytes 131088 | tf_op jit(solution)/shard_map/reduce_scatter | solution.py:36
  102.4 11.6 %all_to_all.18 = f32[16,2,8,128]{3,2,1,0:T(8,128)S(1)} all-to-all(f32[16,2,8,128]{3,2,1,0:T(8,128)} %reduce-scatter.2.cloned.1.call-done), channel_id=1, replica_groups=mesh['grp'=2,'row'=16] {'row'}, dimensions={0} | all-to-all | bytes 262144 | tf_op jit(solution)/shard_map/all_to_all | solution.py:37
  114.0 0.7 slice_bitcast_fusion
  (1 shorter events, 0.0 us)
Async XLA Ops:
  7.2 28.3 %copy-start = (f32[24,128,128]{2,1,0:T(8,128)S(1)}, f32[24,128,128]{2,1,0:T(8,128)}, u32[]{:S(2)}) copy-start(f32[24,128,128]{2,1,0:T(8,128)} %param.8) | copy-start | bytes 4718596
  7.2 95.2 %reduce-scatter.2.cloned.1.call-start = ((), (), s32[]{:S(2)}) async-start(), calls=%async_computation.2 | async-start | bytes 2228224 | tf_op jit(solution)/shard_map/reduce_scatter | solution.py:36
  35.4 1.9 %copy-start.1 = (f32[24,128,128]{2,1,0:T(8,128)S(1)}, f32[24,128,128]{2,1,0:T(8,128)}, u32[]{:S(2)}) copy-start(f32[24,128,128]{2,1,0:T(8,128)} %param.9) | copy-start | bytes 4718596
Sparse Core Ops, SparseCore 0:
  43.3 59.0 reduce-scatter.1
where the time goes:
time: 122 us; the launch traced here: 121 us
  waiting for transfers between devices  59.2 us (49%)
  blocking collectives  34.9 us (29%)
  between operations  14.1 us (12%)
  matrix products  9.08 us (7%)
  local copies, waits for them, and re-layouts  2.51 us (2%)
  other arithmetic  1.66 us (1%)
    reduce_scatter x1, waiting for transfers between devices, shards(): by_rows = lax.psum_scatter(whole, 'row', scatter_dimension=2, tiled=True)  59.2 us
    all_gather x1, blocking collectives, shards(): every_k = lax.all_gather(kmesh, 'row', axis=0, tiled=True)  23.3 us
    all_to_all x1, blocking collectives, shards(): lax.all_to_all(by_rows, 'row', split_axis=0, concat_axis=2, tiled=True)  11.6 us
    dot_general x1, matrix products, phase_terms(): jnp.dot(sine, real_flat, precision=highest, preferred_element_type=jnp.fl...  3.3 us
  transfers between devices with their start and end apart: 1, of which 1 were waited for; matrix products, arithmetic and copies ran while one was open for 0% of the time, Pallas kernels for 0%

commit v1 on v0

--- a/solution.py
+++ b/solution.py
@@ -34,7 +34,15 @@
     part_re, part_im = phase_terms(every_k, rcoord, inverse, real_flat, imag_flat)
     whole = jnp.concatenate([part_re, part_im], axis=1).reshape(total_k, 2, width, width)
     by_rows = lax.psum_scatter(whole, "row", scatter_dimension=2, tiled=True)
-    mine = lax.all_to_all(by_rows, "row", split_axis=0, concat_axis=2, tiled=True)
+    mine = jnp.concatenate(
+        jax.lax.all_to_all(
+            jnp.stack(jnp.split(by_rows, jax.lax.axis_size("row"), 0), 0),
+            axis_name="row",
+            split_axis=0,
+            concat_axis=0,
+        ),
+        2,
+    )
     return (mine[:, 0], mine[:, 1])
 
 

time: 122 us -> 134 us (1.098)
  local copies, waits for them, and re-layouts: 2.51 us -> 13.7 us
    unnamed x5 -> x20, local copies, waits for them, and re-layouts: 1.76 us -> 12.2 us
where the time goes in v1:
time: 134 us; the launch traced here: 132 us
  waiting for transfers between devices  59.2 us (44%)
  blocking collectives  34.7 us (26%)
  between operations  14.1 us (11%)
  local copies, waits for them, and re-layouts  13.7 us (10%)
  matrix products  9.08 us (7%)
  other arithmetic  1.66 us (1%)
    reduce_scatter x1, waiting for transfers between devices, shards(): by_rows = lax.psum_scatter(whole, 'row', scatter_dimension=2, tiled=True)  59.2 us
    all_gather x1, blocking collectives, shards(): every_k = lax.all_gather(kmesh, 'row', axis=0, tiled=True)  23.3 us
    unnamed x20, local copies, waits for them, and re-layouts  12.2 us
    all_to_all x1, blocking collectives, shards(): jax.lax.all_to_all(jnp.stack(jnp.split(by_rows, jax.lax.axis_size('row'),...  11.4 us
    dot_general x1, matrix products, phase_terms(): jnp.dot(sine, real_flat, precision=highest, preferred_element_type=jnp.fl...  3.3 us
  transfers between devices with their start and end apart: 1, of which 1 were waited for; matrix products, arithmetic and copies ran while one was open for 0% of the time, Pallas kernels for 0%

profile of v1, /device:TPU:0, one launch (start us, length us, event | category | flops | bytes accessed | tf_op | source)
XLA Modules:
  0.0 132.4 jit_solution(6939908510027072813)
XLA Ops:
  7.2 0.0 copy-start
  7.2 0.0 reduce-scatter.2.cloned.1.call-start
  7.2 0.8 convert_divide_fusion
  8.0 23.3 %all-gather = s32[16,1,3]{2,1,0:T(1,128)S(1)} all-gather(s32[1,1,3]{2,1,0:T(1,128)} %bitcast.97), channel_id=1, replica_groups=mesh['grp'=2,'row'=16] {'row'}, dimensions={0}, use_global_device_ids=true | all-gather | bytes 204 | tf_op jit(solution)/shard_map/all_gather | solution.py:28
  31.3 0.1 copy.15
  31.4 0.8 multiply_reduce_fusion
  32.1 3.3 %fusion.2 = f32[16,16384]{1,0:T(8,128)S(1)} fusion(f32[3,8,128,128]{3,2,1,0:T(8,128)} %bitcast.92, f32[24]{0:T(128)S(1)} %convert_divide_fusion, s32[16,24]{1,0:T(8,128)S(1)} %multiply_reduce_fusion), kind=kOutput, calls=%fused_computation.5 | convolution fusion | flops 75502848 | bytes 2623072 | tf_op jit(solution)/shard_map/dot_general | solution.py:20
  35.4 0.0 copy-done
  35.4 0.0 copy-start.1
  35.4 1.9 %fusion.4 = f32[16,16384]{1,0:T(8,128)S(1)} fusion(f32[3,8,128,128]{3,2,1,0:T(8,128)S(1)} %bitcast.93, f32[24]{0:T(128)S(1)} %convert_divide_fusion, s32[16,24]{1,0:T(8,128)S(1)} %multiply_reduce_fusion), kind=kOutput, calls=%fused_computation.7 | convolution fusion | flops 75502848 | bytes 2623072 | tf_op jit(solution)/shard_map/dot_general | solution.py:17
  37.4 0.0 copy-done.1
  37.4 1.9 %convolution_add_fusion = f32[16,16384]{1,0:T(8,128)S(1)} fusion(f32[16,16384]{1,0:T(8,128)S(1)} %fusion.2, f32[3,8,128,128]{3,2,1,0:T(8,128)S(1)} %bitcast.94, f32[24]{0:T(128)S(1)} %convert_divide_fusion, s32[16,24]{1,0:T(8,128)S(1)} %multiply_reduce_fusion), kind=kOutput, calls=%fused_computation | convolution fusion | flops 75764992 | bytes 3671648 | tf_op jit(solution)/shard_map/dot_general | solution.py:22
  39.3 1.9 %convolution_subtract_fusion = f32[16,16384]{1,0:T(8,128)S(1)} fusion(f32[16,16384]{1,0:T(8,128)S(1)} %fusion.4, f32[3,8,128,128]{3,2,1,0:T(8,128)S(1)} %bitcast.95, f32[24]{0:T(128)S(1)} %convert_divide_fusion, s32[16,24]{1,0:T(8,128)S(1)} %multiply_reduce_fusion), kind=kOutput, calls=%fused_computation.1 | convolution fusion | flops 75764992 | bytes 3671648 | tf_op jit(solution)/shard_map/dot_general | solution.py:19
  41.2 0.1 maximum_bitcast_fusion
  41.4 1.8 %copy.19 = f32[2,8,256,128]{3,2,1,0:T(8,128)} copy(f32[2,8,256,128]{3,1,2,0:T(8,128)S(1)} %maximum_bitcast_fusion) | data formatting | bytes 4194304
  43.1 0.0 reduce-scatter.2.cloned.1.call-update
  43.2 59.2 %reduce-scatter.2.cloned.1.call-done = f32[16,2,8,128]{3,2,1,0:T(8,128)} async-done(((f32[16,2,128,128]{3,2,1,0:T(8,128)}), f32[16,2,8,128]{3,2,1,0:T(8,128)}) %reduce-scatter.2.cloned.1.call-update) | async-done | bytes 131088 | tf_op jit(solution)/shard_map/reduce_scatter | solution.py:36
  102.4 0.7 constant_dynamic-update-slice_fusion.15
  103.1 0.7 constant_dynamic-update-slice_fusion.14
  103.8 0.7 constant_dynamic-update-slice_fusion.13
  104.5 0.7 constant_dynamic-update-slice_fusion.12
  105.2 0.7 constant_dynamic-update-slice_fusion.11
  105.9 0.7 constant_dynamic-update-slice_fusion.10
  106.6 0.7 constant_dynamic-update-slice_fusion.9
  107.3 0.7 constant_dynamic-update-slice_fusion.8
  108.0 0.7 constant_dynamic-update-slice_fusion.7
  108.7 0.7 constant_dynamic-update-slice_fusion.6
  109.4 0.7 constant_dynamic-update-slice_fusion.5
  110.1 0.7 constant_dynamic-update-slice_fusion.4
  110.8 0.7 constant_dynamic-update-slice_fusion.3
  111.5 0.7 constant_dynamic-update-slice_fusion.2
  112.2 0.7 constant_dynamic-update-slice_fusion.1
  112.9 0.7 constant_dynamic-update-slice_fusion
  113.6 11.4 %all_to_all.5 = f32[16,1,2,8,128]{4,3,2,1,0:T(8,128)S(1)} all-to-all(f32[16,1,2,8,128]{4,3,2,1,0:T(8,128)S(1)} %constant_dynamic-update-slice_fusion), channel_id=1, replica_groups=mesh['grp'=2,'row'=16] {'row'}, dimensions={0} | all-to-all | bytes 262144 | tf_op jit(solution)/shard_map/all_to_all | solution.py:38
  124.9 0.7 slice_bitcast_fusion
  (1 shorter events, 0.0 us)
Async XLA Ops:
  7.2 28.3 %copy-start = (f32[24,128,128]{2,1,0:T(8,128)S(1)}, f32[24,128,128]{2,1,0:T(8,128)}, u32[]{:S(2)}) copy-start(f32[24,128,128]{2,1,0:T(8,128)} %param.8) | copy-start | bytes 4718596
  7.2 95.2 %reduce-scatter.2.cloned.1.call-start = ((), (), s32[]{:S(2)}) async-start(), calls=%async_computation.2 | async-start | bytes 2228224 | tf_op jit(solution)/shard_map/reduce_scatter | solution.py:36
  35.4 1.9 %copy-start.1 = (f32[24,128,128]{2,1,0:T(8,128)S(1)}, f32[24,128,128]{2,1,0:T(8,128)}, u32[]{:S(2)}) copy-start(f32[24,128,128]{2,1,0:T(8,128)} %param.9) | copy-start | bytes 4718596
Sparse Core Ops, SparseCore 0:
  43.3 59.0 reduce-scatter.1
